TPU v7x, 32 devices: a whole 2x2x4 slice. The times are simulated.
32 devices in a mesh: ctx: 4 (over y, x), fsdp: 8 (over z, core).
Axes of the slice: x: 2, y: 2, z: 4, core: 2. Of those that a mesh axis runs over, the one named last changes fastest.
Arguments:
- layer_input: bfloat16 [1280, 4, 1536], P(('ctx', 'fsdp')), may hold values from -6 to 6
- block_order: int32 [2, 8], replicated, may hold values from 0 to 7, each once within a row
- first_gain: bfloat16 [1536], P('fsdp'), may hold values from 0.25 to 1.75
- w_qkv: bfloat16 [1536, 2048], P('fsdp'), may hold values from -0.15625 to 0.15625
- b_qkv: bfloat16 [2048], P('fsdp'), may hold values from -1.5 to 1.5
- w_o: bfloat16 [1536, 1536], P('fsdp'), may hold values from -1.25 to 1.25
- second_gain: bfloat16 [1536], P('fsdp'), may hold values from 0.25 to 1.75
- w_gate: bfloat16 [1536, 8960], P('fsdp'), may hold values from -0.15625 to 0.15625
- w_up: bfloat16 [1536, 8960], P('fsdp'), may hold values from -0.15625 to 0.15625
- w_down: bfloat16 [8960, 1536], P('fsdp'), may hold values from -0.0625 to 0.0625
- cotangent: bfloat16 [1280, 4, 1536], P(('ctx', 'fsdp')), may hold values from -6 to 6
Outputs:
- mixed: bfloat16 [1280, 4, 1536], P(('ctx', 'fsdp'))
- input_grad: float32 [1280, 4, 1536], P(('ctx', 'fsdp'))
- first_gain_grad: float32 [1536], P('fsdp')
- w_qkv_grad: float32 [1536, 2048], P('fsdp')
- b_qkv_grad: float32 [1792], P('fsdp')
- value_bias_grad: float32 [256], P('fsdp')
- w_o_grad: float32 [1536, 1536], P('fsdp')
- second_gain_grad: float32 [1536], P('fsdp')
- w_gate_grad: float32 [1536, 8960], P('fsdp')
- w_up_grad: float32 [1536, 8960], P('fsdp')
- w_down_grad: float32 [8960, 1536], P('fsdp')
Inputs may be any that keep to these rules, and one draw needn't show every extreme that they name: `block_order`: each row is a permutation.
All inputs are finite; a program needn't handle non-finite values.
Results may differ from a plain program's by a relative error of at most 0.02.
Values may be sent and summed in bfloat16 or wider, within the bound.
A program may use at most 576 MiB of HBM per device.

v0:
```python
import math
import jax
import jax.numpy as jnp
from jax import lax
from jax.sharding import PartitionSpec as P

D = 1536
H = 12
KVH = 2
HD = 128
FF = 8960
SEQS = 2
QKV = 2048
QK = 1792
EPS = 1e-06
THETA = 1000000.0
KEY_BLOCK = 256
NEG_FILL = -1e30
CONTRACT_LAST = (((1,), (1,)), ((), ()))
CONTRACT_FIRST = (((0,), (0,)), ((), ()))


def narrowed(values):
    return lax.optimization_barrier(values.astype(jnp.bfloat16)).astype(jnp.float32)


def block_positions(block_order, first_row, row_count, block_rows, ctx_size):
    row_index = first_row + jnp.arange(row_count, dtype=jnp.int32)
    slot_index = jnp.arange(2 * SEQS, dtype=jnp.int32)
    entries = (slot_index // SEQS)[None, :] * ctx_size + (row_index // block_rows)[:, None]
    tiled = jnp.tile(block_order, (2, 1))
    entry_ids = jnp.arange(2 * ctx_size, dtype=jnp.int32)
    picked = jnp.sum(
        jnp.where(entries[:, :, None] == entry_ids[None, None, :], tiled[None, :, :], 0), -1
    )
    return picked * block_rows + (row_index % block_rows)[:, None]


def pos_groups(positions):
    row_count = positions.shape[0]
    return positions.reshape(row_count, 2, SEQS).transpose(2, 0, 1).reshape(SEQS, row_count * 2)


def to_groups(tokens, row_count, group_size):
    shaped = tokens.reshape(row_count, 2, SEQS, KVH, group_size, HD)
    return shaped.transpose(2, 3, 4, 0, 1, 5).reshape(SEQS, KVH, group_size * row_count * 2, HD)


def from_groups(grouped, row_count, group_size):
    shaped = grouped.reshape(SEQS, KVH, group_size, row_count, 2, HD).transpose(3, 4, 0, 1, 2, 5)
    return shaped.reshape(row_count * 2 * SEQS, KVH * group_size * HD)


def rope_tables(positions):
    half_width = HD // 2
    frequency = THETA ** (-jnp.arange(half_width, dtype=jnp.float32) * 2.0 / HD)
    angles = positions.astype(jnp.float32)[:, None] * frequency[None, :]
    cosine_table = jnp.concatenate([jnp.cos(angles), jnp.cos(angles)], -1)[:, None, :]
    sine_table = jnp.concatenate([jnp.sin(angles), jnp.sin(angles)], -1)[:, None, :]
    return (cosine_table, sine_table)


def rotate(head_values, cosine_table, sine_table):
    half_width = HD // 2
    turned = jnp.concatenate([-head_values[..., half_width:], head_values[..., :half_width]], -1)
    return head_values * cosine_table + turned * sine_table


def rotate_back(grad_values, cosine_table, sine_table):
    half_width = HD // 2
    moved = grad_values * sine_table
    return grad_values * cosine_table + jnp.concatenate(
        [moved[..., half_width:], -moved[..., :half_width]], -1
    )


def normalize(values, gain):
    scale = lax.rsqrt(jnp.mean(values * values, -1, keepdims=True) + EPS)
    unit = values * scale
    return (unit, scale, unit * gain)


def norm_back(grad_out, unit, scale, gain):
    grad_unit = grad_out * gain
    inner = jnp.mean(grad_unit * unit, -1, keepdims=True)
    return (scale * (grad_unit - unit * inner), jnp.sum(grad_out * unit, 0))


def split_blocks(piece):
    row_count = piece.shape[0]
    size = math.gcd(row_count, KEY_BLOCK)
    stacked = piece.reshape(row_count // size, size, piece.shape[1], piece.shape[2])
    firsts = size * jnp.arange(row_count // size, dtype=jnp.int32)
    return (stacked, firsts)


def shards(
    layer_input,
    block_order,
    first_gain,
    w_qkv,
    b_qkv,
    w_o,
    second_gain,
    w_gate,
    w_up,
    w_down,
    cotangent,
):
    ctx_size = lax.axis_size("ctx")
    shard_count = lax.axis_size("fsdp")
    rows_here = layer_input.shape[0]
    slots = layer_input.shape[1]
    block_rows = rows_here * shard_count
    group_size = H // KVH
    kv_width = KVH * HD
    first_row = (lax.axis_index("ctx") * shard_count + lax.axis_index("fsdp")) * rows_here
    own_pos = block_positions(block_order, first_row, rows_here, block_rows, ctx_size)
    cosine_table, sine_table = rope_tables(own_pos.reshape(-1))
    query_scale = HD ** (-0.5)
    w_qkv_all, w_o_all, bias_all, gain_one, gain_two = (
        lax.all_gather(w_qkv, "fsdp", axis=0, tiled=True),
        lax.all_gather(w_o, "fsdp", axis=0, tiled=True),
        lax.all_gather(b_qkv, "fsdp", axis=0, tiled=True),
        lax.all_gather(first_gain, "fsdp", axis=0, tiled=True),
        lax.all_gather(second_gain, "fsdp", axis=0, tiled=True),
    )
    gain_one = gain_one.astype(jnp.float32)
    gain_two = gain_two.astype(jnp.float32)
    inputs = layer_input.reshape(-1, D).astype(jnp.float32)
    unit_one, scale_one, normed = normalize(inputs, gain_one)
    normed_one = normed.astype(jnp.bfloat16)
    projected = jnp.dot(
        normed_one, w_qkv_all, preferred_element_type=jnp.float32
    ) + bias_all.astype(jnp.float32)
    query_raw = projected[:, : H * HD].reshape(-1, H, HD)
    key_raw = projected[:, H * HD : H * HD + kv_width].reshape(-1, KVH, HD)
    value_raw = projected[:, H * HD + kv_width :]
    query_tokens = (
        (rotate(query_raw, cosine_table, sine_table) * query_scale)
        .astype(jnp.bfloat16)
        .reshape(-1, H * HD)
    )
    key_tokens = (
        rotate(key_raw, cosine_table, sine_table).astype(jnp.bfloat16).reshape(-1, kv_width)
    )
    own_kv = jnp.concatenate([key_tokens, value_raw.astype(jnp.bfloat16)], -1).reshape(
        rows_here, slots, 2 * kv_width
    )
    block_kv = lax.all_gather(own_kv, "fsdp", axis=0, tiled=True)
    queries = to_groups(query_tokens, rows_here, group_size)
    query_pos = jnp.tile(pos_groups(own_pos), (1, group_size))
    query_count = queries.shape[2]

    def piece_keys(key_rows, row_start):
        row_count = key_rows.shape[0]
        flat = key_rows.reshape(row_count * slots, 2 * kv_width)
        keys_grouped = to_groups(flat[:, :kv_width], row_count, 1)
        values_grouped = to_groups(flat[:, kv_width:], row_count, 1)
        key_pos = pos_groups(
            block_positions(block_order, row_start, row_count, block_rows, ctx_size)
        )
        visible = query_pos[:, None, :, None] >= key_pos[:, None, None, :]
        scores = jnp.einsum(
            "snmd,snkd->snmk", queries, keys_grouped, preferred_element_type=jnp.float32
        )
        return (keys_grouped, values_grouped, visible, scores)

    start_state = (
        jnp.full((SEQS, KVH, query_count), NEG_FILL, jnp.float32),
        jnp.zeros((SEQS, KVH, query_count), jnp.float32),
        jnp.zeros((SEQS, KVH, query_count, HD), jnp.float32),
    )
    state = start_state
    stacked, firsts = split_blocks(lax.all_gather(block_kv, "ctx", axis=0, tiled=True))

    def forward_one_block(carry, item):
        best, totals, accum = carry
        key_rows, row_start = item
        keys_grouped, values_grouped, visible, scores = piece_keys(key_rows, row_start)
        scores = jnp.where(visible, scores, NEG_FILL)
        fresh = jnp.maximum(best, jnp.max(scores, -1))
        weights = jnp.where(visible, jnp.exp(scores - fresh[..., None]), 0.0)
        decay = jnp.exp(best - fresh)
        totals = totals * decay + jnp.sum(weights, -1)
        accum = accum * decay[..., None] + jnp.einsum(
            "snmk,snkd->snmd",
            weights.astype(jnp.bfloat16),
            values_grouped,
            preferred_element_type=jnp.float32,
        )
        return ((fresh, totals, accum), None)

    state, unused = lax.scan(forward_one_block, state, (stacked, firsts))
    best, totals, accum = state
    attended_grouped = accum / totals[..., None]
    logsum = best + jnp.log(totals)
    attended_low = from_groups(attended_grouped, rows_here, group_size).astype(jnp.bfloat16)
    middle = inputs + jnp.dot(attended_low, w_o_all, preferred_element_type=jnp.float32)
    unit_two, scale_two, normed = normalize(middle, gain_two)
    normed_two = normed.astype(jnp.bfloat16)
    gate_all, up_all, down_all = (
        lax.all_gather(w_gate, "fsdp", axis=0, tiled=True),
        lax.all_gather(w_up, "fsdp", axis=0, tiled=True),
        lax.all_gather(w_down, "fsdp", axis=0, tiled=True),
    )
    gate_part = jnp.dot(normed_two, gate_all, preferred_element_type=jnp.float32)
    up_part = jnp.dot(normed_two, up_all, preferred_element_type=jnp.float32)
    activated = jax.nn.silu(gate_part)
    hidden = (activated * up_part).astype(jnp.bfloat16)
    mixed_out = middle + jnp.dot(hidden, down_all, preferred_element_type=jnp.float32)
    output = mixed_out.astype(jnp.bfloat16).reshape(rows_here, slots, D)
    gate_all, up_all, down_all = (
        lax.all_gather(w_gate, "fsdp", axis=0, tiled=True),
        lax.all_gather(w_up, "fsdp", axis=0, tiled=True),
        lax.all_gather(w_down, "fsdp", axis=0, tiled=True),
    )
    w_qkv_all, w_o_all = (
        lax.all_gather(w_qkv, "fsdp", axis=0, tiled=True),
        lax.all_gather(w_o, "fsdp", axis=0, tiled=True),
    )
    grad_branch_two = cotangent.reshape(-1, D)
    grad_hidden = lax.dot_general(
        grad_branch_two, down_all, CONTRACT_LAST, preferred_element_type=jnp.float32
    )
    sigmoid_gate = jax.nn.sigmoid(gate_part)
    grad_gate = grad_hidden * up_part * sigmoid_gate * (1.0 + gate_part * (1.0 - sigmoid_gate))
    grad_gate_up = jnp.concatenate([grad_gate, grad_hidden * activated], -1).astype(jnp.bfloat16)
    grad_normed_two = lax.dot_general(
        grad_gate_up[:, :FF], gate_all, CONTRACT_LAST, preferred_element_type=jnp.float32
    )
    grad_normed_two = grad_normed_two + lax.dot_general(
        grad_gate_up[:, FF:], up_all, CONTRACT_LAST, preferred_element_type=jnp.float32
    )
    grad_middle_norm, grad_gain_two = norm_back(grad_normed_two, unit_two, scale_two, gain_two)
    grad_middle = cotangent.reshape(-1, D).astype(jnp.float32) + grad_middle_norm
    grad_branch_one = grad_middle.astype(jnp.bfloat16)
    grad_attended = lax.dot_general(
        grad_branch_one, w_o_all, CONTRACT_LAST, preferred_element_type=jnp.float32
    ).astype(jnp.bfloat16)
    grad_out_grouped = to_groups(grad_attended, rows_here, group_size)
    delta = jnp.sum(grad_out_grouped.astype(jnp.float32) * attended_grouped, -1)
    back_state = (
        jnp.zeros((SEQS, KVH, query_count, HD), jnp.float32),
        jnp.zeros((ctx_size * block_rows, slots, 2 * kv_width), jnp.float32),
    )
    state = back_state
    stacked, firsts = split_blocks(lax.all_gather(block_kv, "ctx", axis=0, tiled=True))

    def backward_one_block(carry, item):
        grad_queries, grad_kv_full = carry
        key_rows, row_start = item
        row_count = key_rows.shape[0]
        keys_grouped, values_grouped, visible, scores = piece_keys(key_rows, row_start)
        probs = jnp.where(
            visible, jnp.exp(jnp.where(visible, scores, NEG_FILL) - logsum[..., None]), 0.0
        )
        grad_probs = jnp.einsum(
            "snmd,snkd->snmk", grad_out_grouped, values_grouped, preferred_element_type=jnp.float32
        )
        grad_scores = (probs * (grad_probs - delta[..., None])).astype(jnp.bfloat16)
        grad_queries = grad_queries + jnp.einsum(
            "snmk,snkd->snmd", grad_scores, keys_grouped, preferred_element_type=jnp.float32
        )
        grad_keys = jnp.einsum(
            "snmk,snmd->snkd", grad_scores, queries, preferred_element_type=jnp.float32
        )
        grad_values = jnp.einsum(
            "snmk,snmd->snkd",
            probs.astype(jnp.bfloat16),
            grad_out_grouped,
            preferred_element_type=jnp.float32,
        )
        block_terms = jnp.concatenate(
            [from_groups(grad_keys, row_count, 1), from_groups(grad_values, row_count, 1)], -1
        ).reshape(row_count, slots, 2 * kv_width)
        previous = lax.dynamic_slice_in_dim(grad_kv_full, row_start, row_count, 0)
        grad_kv_full = lax.dynamic_update_slice_in_dim(
            grad_kv_full, previous + block_terms, row_start, 0
        )
        return ((grad_queries, grad_kv_full), None)

    state, unused = lax.scan(backward_one_block, state, (stacked, firsts))
    grad_queries, grad_kv_full = state
    grad_kv = lax.psum_scatter(grad_kv_full, ("ctx", "fsdp"), scatter_dimension=0, tiled=True)
    grad_kv_low = narrowed(grad_kv).reshape(-1, 2 * kv_width)
    grad_query_tokens = from_groups(narrowed(grad_queries), rows_here, group_size) * query_scale
    grad_query_raw = rotate_back(
        grad_query_tokens.reshape(-1, H, HD), cosine_table, sine_table
    ).reshape(-1, H * HD)
    grad_key_raw = rotate_back(
        grad_kv_low[:, :kv_width].reshape(-1, KVH, HD), cosine_table, sine_table
    ).reshape(-1, kv_width)
    grad_projected = jnp.concatenate(
        [grad_query_raw, grad_key_raw, grad_kv_low[:, kv_width:]], -1
    ).astype(jnp.bfloat16)
    grad_bias = jnp.sum(grad_projected, 0, dtype=jnp.float32)
    grad_bias_qk = grad_bias[:QK]
    grad_bias_value = grad_bias[QK:]
    grad_normed_one = lax.dot_general(
        grad_projected, w_qkv_all, CONTRACT_LAST, preferred_element_type=jnp.float32
    )
    grad_input_norm, grad_gain_one = norm_back(grad_normed_one, unit_one, scale_one, gain_one)
    grad_input = (grad_middle + grad_input_norm).reshape(rows_here, slots, D)
    weight_rows = lax.psum_scatter(
        jnp.concatenate(
            [
                lax.dot_general(
                    normed_two, grad_gate_up, CONTRACT_FIRST, preferred_element_type=jnp.float32
                ),
                lax.dot_general(
                    normed_one, grad_projected, CONTRACT_FIRST, preferred_element_type=jnp.float32
                ),
                lax.dot_general(
                    attended_low,
                    grad_branch_one,
                    CONTRACT_FIRST,
                    preferred_element_type=jnp.float32,
                ),
            ],
            1,
        ).astype(jnp.bfloat16),
        "fsdp",
        scatter_dimension=0,
        tiled=True,
    ).astype(jnp.float32)
    down_rows = lax.psum_scatter(
        lax.dot_general(
            hidden, grad_branch_two, CONTRACT_FIRST, preferred_element_type=jnp.float32
        ).astype(jnp.bfloat16),
        "fsdp",
        scatter_dimension=0,
        tiled=True,
    ).astype(jnp.float32)
    gain_one_rows, gain_two_rows, bias_rows, value_bias_rows = (
        lax.psum_scatter(grad_gain_one, "fsdp", scatter_dimension=0, tiled=True),
        lax.psum_scatter(grad_gain_two, "fsdp", scatter_dimension=0, tiled=True),
        lax.psum_scatter(grad_bias_qk, "fsdp", scatter_dimension=0, tiled=True),
        lax.psum_scatter(grad_bias_value, "fsdp", scatter_dimension=0, tiled=True),
    )
    weight_rows, down_rows, gain_one_rows, gain_two_rows, bias_rows, value_bias_rows = (
        lax.psum(weight_rows.astype(jnp.bfloat16), "ctx").astype(jnp.float32),
        lax.psum(down_rows.astype(jnp.bfloat16), "ctx").astype(jnp.float32),
        lax.psum(gain_one_rows.astype(jnp.bfloat16), "ctx").astype(jnp.float32),
        lax.psum(gain_two_rows.astype(jnp.bfloat16), "ctx").astype(jnp.float32),
        lax.psum(bias_rows.astype(jnp.bfloat16), "ctx").astype(jnp.float32),
        lax.psum(value_bias_rows.astype(jnp.bfloat16), "ctx").astype(jnp.float32),
    )
    return (
        output,
        grad_input,
        gain_one_rows,
        weight_rows[:, 2 * FF : 2 * FF + QKV],
        bias_rows,
        value_bias_rows,
        weight_rows[:, 2 * FF + QKV :],
        gain_two_rows,
        weight_rows[:, :FF],
        weight_rows[:, FF : 2 * FF],
        down_rows,
    )


def solution(mesh):
    in_specs = (
        P(("ctx", "fsdp"), None, None),
        P(),
        P("fsdp"),
        P("fsdp", None),
        P("fsdp"),
        P("fsdp", None),
        P("fsdp"),
        P("fsdp", None),
        P("fsdp", None),
        P("fsdp", None),
        P(("ctx", "fsdp"), None, None),
    )
    out_specs = (
        P(("ctx", "fsdp"), None, None),
        P(("ctx", "fsdp"), None, None),
        P("fsdp"),
        P("fsdp", None),
        P("fsdp"),
        P("fsdp"),
        P("fsdp", None),
        P("fsdp"),
        P("fsdp", None),
        P("fsdp", None),
        P("fsdp", None),
    )
    return jax.shard_map(shards, mesh=mesh, in_specs=in_specs, out_specs=out_specs, check_vma=False)
```

profile of v0, /device:TPU:0, one launch (start us, length us, event | category | flops | bytes accessed | tf_op | source)
XLA Modules:
  0.0 2331.6 jit_solution(8139246037101609936)
XLA Ops:
  9.8 13.5 all-gather
  27.0 15.6 all-reduce.8
  46.4 31.2 %all-gather.9.cloned.1.call-done = bf16[1536,2048]{1,0:T(8,128)(2,1)} async-done(((bf16[192,2048]{1,0:T(8,128)(2,1)}), bf16[1536,2048]{1,0:T(8,128)(2,1)}) %all-gather.9.cloned.1.call-update) | async-done | bytes 6291472 | tf_op jit(solution)/shard_map/all_gather | solution.py:122
  84.0 22.2 all-gather.11.cloned.1.call-done
  125.7 43.1 %all-gather.13.cloned.1.call-done = bf16[1280,4,512]{2,1,0:T(4,128)(2,1)} async-done(((bf16[320,4,512]{2,1,0:T(4,128)(2,1)}), bf16[1280,4,512]{2,1,0:T(4,128)(2,1)}) %all-gather.13.cloned.1.call-update) | async-done | bytes 5242896 | tf_op jit(solution)/shard_map/all_gather | solution.py:175
  168.8 82.5 %while.34 = (s32[]{:T(128)}, f32[2,2,480]{2,1,0:T(2,128)S(1)}, f32[2,2,480]{2,1,0:T(2,128)S(1)}, f32[2,2,480,128]{3,2,1,0:T(8,128)}, s32[5]{0:T(128)S(1)}, /*ind...) while((s32[]{:T(128)}, f32[2,2,480]{2,1,0:T(2,128)S(1)}, ...), condition=%wide.region_6.7_spmd.clone, body=%wide.region_2.6_spmd.clone.sunk | while | flops 514415264 | bytes 27955316 | solution.py:194
  257.4 203.6 %all-gather.17.cloned.1.call-done = bf16[1536,8960]{1,0:T(8,128)(2,1)} async-done(((bf16[192,8960]{1,0:T(8,128)(2,1)}), bf16[1536,8960]{1,0:T(8,128)(2,1)}) %all-gather.17.cloned.1.call-update) | async-done | bytes 27525136 | tf_op jit(solution)/shard_map/all_gather | solution.py:203
  461.0 16.3 fusion.69
  477.3 222.6 %all-gather.19.cloned.1.call-done = bf16[1536,8960]{1,0:T(8,128)(2,1)} async-done(((bf16[192,8960]{1,0:T(8,128)(2,1)}), bf16[1536,8960]{1,0:T(8,128)(2,1)}) %all-gather.19.cloned.1.call-update) | async-done | bytes 27525136 | tf_op jit(solution)/shard_map/all_gather | solution.py:204
  699.9 16.4 fusion.70
  716.4 222.6 %all-gather.21.cloned.1.call-done = bf16[8960,1536]{1,0:T(8,128)(2,1)} async-done(((bf16[1120,1536]{1,0:T(8,128)(2,1)}), bf16[8960,1536]{1,0:T(8,128)(2,1)}) %all-gather.21.cloned.1.call-update) | async-done | bytes 27525136 | tf_op jit(solution)/shard_map/all_gather | solution.py:205
  939.0 19.8 multiply_convert_fusion
  958.8 15.2 convolution_convert_fusion.1
  974.0 17.0 fusion.71
  991.0 16.1 multiply_reduce_fusion
  1019.8 165.6 %while.35 = (s32[]{:T(128)}, f32[2,2,480,128]{3,2,1,0:T(8,128)}, f32[1280,4,512]{2,1,0:T(4,128)}, s32[5]{0:T(128)S(1)}, s32[2,8]{1,0:T(2,128)S(1)}, /*index=5*/b...) while((s32[]{:T(128)}, f32[2,2,480,128]{3,2,1,0:T(8,128)}, ...), condition=%wide.region_12.13_spmd.clone, body=%wide.region_10.12_spmd.clone.sunk | while | flops 1270183168 | bytes 55970532 | solution.py:283
  1188.1 176.6 %all-reduce.15 = bf16[1280,4,512]{2,1,0:T(4,128)(2,1)} all-reduce(f32[1280,4,512]{2,1,0:T(4,128)} %get-tuple-element.344), channel_id=2, replica_groups=mesh['ctx'=4,'fsdp'=8] {'ctx','fsdp'}, use_global_device_ids=true, to_apply=%region_13.14.clone | all-reduce | flops 2621440 | bytes 15728640
  1380.7 23.8 %convolution_convert_fusion = bf16[1536,17920]{1,0:T(8,128)(2,1)} fusion(bf16[160,1536]{1,0:T(8,128)(2,1)S(1)} %copy-done.10, bf16[160,8960]{1,0:T(8,128)(2,1)} %get-tuple-element.485, bf16[160,8960]{1,0:T(8,128)(2,1)} %get-tuple-element.486), kind=kOutput, calls=%fused_computation.72 | convolution fusion | flops 8847032320 | bytes 61276160 | tf_op jit(solution)/shard_map/dot_general | solution.py:308
  1404.5 44.2 %pad_maximum_fusion = bf16[1536,21504]{1,0:T(8,128)(2,1)} fusion(bf16[1536,1536]{1,0:T(8,128)(2,1)} %convolution_convert_fusion.3, bf16[1536,2048]{1,0:T(8,128)(2,1)} %convolution_convert_fusion.2, bf16[1536,17920]{1,0:T(8,128)(2,1)} %convolution_convert_fusion), kind=kLoop, calls=%fused_computation.73 | loop fusion | flops 198180864 | bytes 132120576 | tf_op jit(solution)/shard_map/concatenate | solution.py:306
  1448.8 629.6 %reduce-scatter.3.cloned.1.call-done = bf16[192,21504]{1,0:T(8,128)(2,1)} async-done(((bf16[1536,21504]{1,0:T(8,128)(2,1)}), bf16[192,21504]{1,0:T(8,128)(2,1)}) %reduce-scatter.3.cloned.1.call-update) | async-done | bytes 8257552 | tf_op jit(solution)/shard_map/reduce_scatter | solution.py:305
  2080.4 16.4 fusion.44
  2107.0 26.1 %all-reduce.7 = (bf16[1536]{0:T(1024)(128)(2,1)S(1)}, bf16[1792]{0:T(1024)(128)(2,1)S(1)}, bf16[256]{0:T(256)(128)(2,1)S(1)}, bf16[1536]{0:T(1024)(128)(2,1)S(1)}) all-reduce(f32[1536]{0:T(1024)S(1)} %get-tuple-element.419, f32[1792]{0:T(1024)S(1)} %bitcast.253, ...), channel_id=3, replica_groups=mesh['ctx'=4,'fsdp'=8] {'fsdp'}, use_global_device_ids=true, to_apply=%region_16.17.clone | all-reduce | flops 5120 | bytes 30720
  2133.4 10.2 all-reduce.9
  2145.9 160.7 %all-reduce.14.cloned.1.call-done = (bf16[192,21504]{1,0:T(8,128)(2,1)}, bf16[1120,1536]{1,0:T(8,128)(2,1)}) async-done(((bf16[192,21504]{1,0:T(8,128)(2,1)}, bf16[1120,1536]{1,0:T(8,128)(2,1)}), (bf16[192,21504]{1,0:T(8,128)(2,1)}, bf16[1120,1536]{1,0:T(8,128)(2,1)})) %all-reduce.14.cloned.1.call-update) | async-done | bytes 11698192 | tf_op jit(solution)/shard_map/psum | solution.py:342
  (512 shorter events, 339.1 us)
Async XLA Ops:
  7.2 70.4 %all-gather.9.cloned.1.call-start = ((), (), s32[]{:S(2)}) async-start(), calls=%async_computation.2 | async-start | bytes 7077888 | tf_op jit(solution)/shard_map/all_gather | solution.py:122
  7.9 98.2 %all-gather.11.cloned.1.call-start = ((), (), s32[]{:S(2)}) async-start(), calls=%async_computation.3 | async-start | bytes 1474560 | tf_op jit(solution)/shard_map/all_gather | solution.py:150
  9.1 72.6 %copy-start = (f32[160,1536]{1,0:T(8,128)}, f32[160,1536]{1,0:T(8,128)S(1)}, u32[]{:S(2)}) copy-start(f32[160,1536]{1,0:T(8,128)S(1)} %reshape.608) | copy-start | bytes 2949124
  42.6 39.1 %copy-start.29 = (f32[1536]{0:T(1024)}, f32[1536]{0:T(1024)S(1)}, u32[]{:S(2)}) copy-start(f32[1536]{0:T(1024)S(1)} %convert_element_type.151) | copy-start | bytes 18436
  44.1 33.6 %copy-start.32 = (f32[160]{0:T(256)}, f32[160]{0:T(256)S(1)}, u32[]{:S(2)}) copy-start(f32[160]{0:T(256)S(1)} %rsqrt.20) | copy-start | bytes 1924
  45.6 36.7 %copy-start.26 = (f32[160,128]{1,0:T(8,128)}, f32[160,128]{1,0:T(8,128)S(1)}, u32[]{:S(2)}) copy-start(f32[160,128]{1,0:T(8,128)S(1)} %pad_maximum_fusion.4) | copy-start | bytes 245764
  46.4 35.7 %copy-start.24 = (f32[160,128]{1,0:T(8,128)}, f32[160,128]{1,0:T(8,128)S(1)}, u32[]{:S(2)}) copy-start(f32[160,128]{1,0:T(8,128)S(1)} %get-tuple-element.501) | copy-start | bytes 245764
  81.7 25.7 %copy-start.13 = (f32[160,2048]{1,0:T(8,128)}, f32[160,2048]{1,0:T(8,128)S(1)}, u32[]{:S(2)}) copy-start(f32[160,2048]{1,0:T(8,128)S(1)} %convolution_add_fusion.4) | copy-start | bytes 3932164
  83.9 84.9 %all-gather.13.cloned.1.call-start = ((), (), s32[]{:S(2)}) async-start(), calls=%async_computation.4 | async-start | bytes 6553600 | tf_op jit(solution)/shard_map/all_gather | solution.py:175
  106.1 147.5 %all-gather.15.cloned.1.call-start = ((), (), s32[]{:S(2)}) async-start(), calls=%async_computation.5 | async-start | bytes 5308416 | tf_op jit(solution)/shard_map/all_gather | solution.py:123
  106.7 354.3 %all-gather.17.cloned.1.call-start = ((), (), s32[]{:S(2)}) async-start(), calls=%async_computation.6 | async-start | bytes 30965760 | tf_op jit(solution)/shard_map/all_gather | solution.py:203
  107.3 592.6 %all-gather.19.cloned.1.call-start = ((), (), s32[]{:S(2)}) async-start(), calls=%async_computation.7 | async-start | bytes 30965760 | tf_op jit(solution)/shard_map/all_gather | solution.py:204
  107.9 831.1 %all-gather.21.cloned.1.call-start = ((), (), s32[]{:S(2)}) async-start(), calls=%async_computation.8 | async-start | bytes 30965760 | tf_op jit(solution)/shard_map/all_gather | solution.py:205
  108.7 1340.1 %reduce-scatter.5.cloned.1.call-start = ((), (), s32[]{:S(2)}) async-start(), calls=%async_computation.10 | async-start | bytes 30965760 | tf_op jit(solution)/shard_map/reduce_scatter | solution.py:327
  116.4 7.4 copy-start.15
  122.0 46.8 %copy-start.31 = (s32[2,8]{1,0:T(2,128)S(1)}, s32[2,8]{1,0:T(2,128)}, u32[]{:S(2)}) copy-start(s32[2,8]{1,0:T(2,128)} %param.16) | copy-start | bytes 196
  257.2 749.9 %copy-start.7 = (f32[160,1536]{1,0:T(8,128)}, f32[160,1536]{1,0:T(8,128)S(1)}, u32[]{:S(2)}) copy-start(f32[160,1536]{1,0:T(8,128)S(1)} %get-tuple-element.513) | copy-start | bytes 2949124
  257.4 442.5 %copy-start.9 = (bf16[160,1536]{1,0:T(8,128)(2,1)}, bf16[160,1536]{1,0:T(8,128)(2,1)S(1)}, u32[]{:S(2)}) copy-start(bf16[160,1536]{1,0:T(8,128)(2,1)S(1)} %multiply_convert_fusion.3) | copy-start | bytes 1474564
  477.3 461.7 %copy-start.16 = (bf16[160,1536]{1,0:T(8,128)(2,1)S(1)}, bf16[160,1536]{1,0:T(8,128)(2,1)}, u32[]{:S(2)}) copy-start(bf16[160,1536]{1,0:T(8,128)(2,1)} %reshape.600) | copy-start | bytes 1474564
  974.0 1104.4 %reduce-scatter.3.cloned.1.call-start = ((), (), s32[]{:S(2)}) async-start(), calls=%async_computation.9 | async-start | bytes 74317824 | tf_op jit(solution)/shard_map/reduce_scatter | solution.py:305
  1008.4 5.8 copy-start.17
  1369.8 5.8 copy-start.23
  1448.7 857.9 %all-reduce.14.cloned.1.call-start = ((), (), s32[]{:S(2)}) async-start(), calls=%async_computation.11 | async-start | bytes 23396352 | tf_op jit(solution)/shard_map/psum | solution.py:342
  2311.2 9.2 copy-start.19
  (29 other events, 90.2 us)
Sparse Core Ops, SparseCore 0:
  9.6 67.9 all-gather.8
  84.0 22.0 all-gather.10
  108.0 60.8 all-gather.12
  170.3 51.1 all-gather.14
  223.1 237.9 all-gather.16
  462.5 237.3 all-gather.18
  701.6 237.3 all-gather.20
  974.1 267.4 reduce-scatter.4
  1448.8 629.5 reduce-scatter.2
  2082.0 224.5 all-reduce.13
where the time goes:
time: 2340 us; the launch traced here: 2330 us
  waiting for transfers between devices  1540 us (66%)
  matrix products  274 us (12%)
  blocking collectives  242 us (10%)
  local copies, waits for them, and re-layouts  128 us (5%)
  other arithmetic  118 us (5%)
    reduce_scatter x1, waiting for transfers between devices, shards(): lax.psum_scatter(jnp.concatenate([lax.dot_general(normed_two, grad_gate_u...  630 us
    all_gather x1, waiting for transfers between devices, shards(): lax.all_gather(w_down, 'fsdp', axis=0, tiled=True)  223 us
    all_gather x1, waiting for transfers between devices, shards(): lax.all_gather(w_up, 'fsdp', axis=0, tiled=True)  223 us
    unnamed x3, blocking collectives  218 us
    all_gather x1, waiting for transfers between devices, shards(): lax.all_gather(w_gate, 'fsdp', axis=0, tiled=True)  204 us
    psum x1, waiting for transfers between devices, shards(): lax.psum(weight_rows.astype(jnp.bfloat16), 'ctx').astype(jnp.float32)  161 us
  transfers between devices with their start and end apart: 10, of which 8 were waited for; matrix products, arithmetic and copies ran while one was open for 20% of the time, Pallas kernels for 0%

commit v1 on v0

--- a/solution.py
+++ b/solution.py
@@ -1,3 +1,4 @@
+import functools
 import math
 import jax
 import jax.numpy as jnp
@@ -18,6 +19,13 @@
 NEG_FILL = -1e30
 CONTRACT_LAST = (((1,), (1,)), ((), ()))
 CONTRACT_FIRST = (((0,), (0,)), ((), ()))
+
+
+def pair_shelves_now(field_in, ax_name):
+    return jnp.sum(lax.all_gather(field_in, ax_name), axis=0)
+
+
+work_the_ticks = functools.partial(pair_shelves_now, ax_name="ctx")
 
 
 def narrowed(values):
@@ -339,7 +347,7 @@
         lax.psum_scatter(grad_bias_value, "fsdp", scatter_dimension=0, tiled=True),
     )
     weight_rows, down_rows, gain_one_rows, gain_two_rows, bias_rows, value_bias_rows = (
-        lax.psum(weight_rows.astype(jnp.bfloat16), "ctx").astype(jnp.float32),
+        work_the_ticks(weight_rows.astype(jnp.bfloat16)).astype(jnp.float32),
         lax.psum(down_rows.astype(jnp.bfloat16), "ctx").astype(jnp.float32),
         lax.psum(gain_one_rows.astype(jnp.bfloat16), "ctx").astype(jnp.float32),
         lax.psum(gain_two_rows.astype(jnp.bfloat16), "ctx").astype(jnp.float32),

time: 2340 us -> 2510 us (1.073)
  waiting for transfers between devices: 1540 us -> 1690 us
    all_gather x0 -> x1, waiting for transfers between devices: none -> 289 us  [pair_shelves_now(): return jnp.sum(lax.all_gather(field_in, ax_name), axis=0)]
    psum x1, waiting for transfers between devices: 161 us -> 26.4 us  [shards(): lax.psum(down_rows.astype(jnp.bfloat16), 'ctx').astype(jnp.float32)]
  transfers between devices with their start and end apart: 10 -> 11, of which waited for: 8 -> 9; matrix products, arithmetic and copies ran while one was open for 20% -> 19% of each run, Pallas kernels for 0% -> 0%
where the time goes in v1:
time: 2510 us; the launch traced here: 2500 us
  waiting for transfers between devices  1690 us (67%)
  matrix products  274 us (11%)
  blocking collectives  243 us (10%)
  other arithmetic  136 us (5%)
  local copies, waits for them, and re-layouts  128 us (5%)
    reduce_scatter x1, waiting for transfers between devices, shards(): lax.psum_scatter(jnp.concatenate([lax.dot_general(normed_two, grad_gate_u...  628 us
    all_gather x1, waiting for transfers between devices, pair_shelves_now(): return jnp.sum(lax.all_gather(field_in, ax_name), axis=0)  289 us
    all_gather x1, waiting for transfers between devices, shards(): lax.all_gather(w_down, 'fsdp', axis=0, tiled=True)  223 us
    all_gather x1, waiting for transfers between devices, shards(): lax.all_gather(w_up, 'fsdp', axis=0, tiled=True)  223 us
    unnamed x3, blocking collectives  219 us
    all_gather x1, waiting for transfers between devices, shards(): lax.all_gather(w_gate, 'fsdp', axis=0, tiled=True)  204 us
  transfers between devices with their start and end apart: 11, of which 9 were waited for; matrix products, arithmetic and copies ran while one was open for 19% of the time, Pallas kernels for 0%

profile of v1, /device:TPU:0, one launch (start us, length us, event | category | flops | bytes accessed | tf_op | source)
XLA Modules:
  0.0 2503.3 jit_solution(18057243863386814175)
XLA Ops:
  27.0 15.6 all-reduce.8
  46.4 31.2 %all-gather.11.cloned.1.call-done = bf16[1536,2048]{1,0:T(8,128)(2,1)} async-done(((bf16[192,2048]{1,0:T(8,128)(2,1)}), bf16[1536,2048]{1,0:T(8,128)(2,1)}) %all-gather.11.cloned.1.call-update) | async-done | bytes 6291472 | tf_op jit(solution)/shard_map/all_gather | solution.py:130
  84.0 22.2 all-gather.13.cloned.1.call-done
  125.7 43.1 %all-gather.15.cloned.1.call-done = bf16[1280,4,512]{2,1,0:T(4,128)(2,1)} async-done(((bf16[320,4,512]{2,1,0:T(4,128)(2,1)}), bf16[1280,4,512]{2,1,0:T(4,128)(2,1)}) %all-gather.15.cloned.1.call-update) | async-done | bytes 5242896 | tf_op jit(solution)/shard_map/all_gather | solution.py:183
  168.8 82.5 %while.34 = (s32[]{:T(128)}, f32[2,2,480]{2,1,0:T(2,128)S(1)}, f32[2,2,480]{2,1,0:T(2,128)S(1)}, f32[2,2,480,128]{3,2,1,0:T(8,128)}, s32[5]{0:T(128)S(1)}, /*ind...) while((s32[]{:T(128)}, f32[2,2,480]{2,1,0:T(2,128)S(1)}, ...), condition=%wide.region_6.7_spmd.clone, body=%wide.region_2.6_spmd.clone.sunk | while | flops 514415264 | bytes 27955316 | solution.py:202
  257.4 203.6 %all-gather.19.cloned.1.call-done = bf16[1536,8960]{1,0:T(8,128)(2,1)} async-done(((bf16[192,8960]{1,0:T(8,128)(2,1)}), bf16[1536,8960]{1,0:T(8,128)(2,1)}) %all-gather.19.cloned.1.call-update) | async-done | bytes 27525136 | tf_op jit(solution)/shard_map/all_gather | solution.py:211
  461.0 16.3 fusion.69
  477.3 222.6 %all-gather.21.cloned.1.call-done = bf16[1536,8960]{1,0:T(8,128)(2,1)} async-done(((bf16[192,8960]{1,0:T(8,128)(2,1)}), bf16[1536,8960]{1,0:T(8,128)(2,1)}) %all-gather.21.cloned.1.call-update) | async-done | bytes 27525136 | tf_op jit(solution)/shard_map/all_gather | solution.py:212
  699.9 16.4 fusion.70
  716.4 222.6 %all-gather.23.cloned.1.call-done = bf16[8960,1536]{1,0:T(8,128)(2,1)} async-done(((bf16[1120,1536]{1,0:T(8,128)(2,1)}), bf16[8960,1536]{1,0:T(8,128)(2,1)}) %all-gather.23.cloned.1.call-update) | async-done | bytes 27525136 | tf_op jit(solution)/shard_map/all_gather | solution.py:213
  939.0 19.8 multiply_convert_fusion
  958.8 15.2 convolution_convert_fusion.1
  974.1 17.0 fusion.71
  991.1 16.1 multiply_reduce_fusion
  1019.8 165.6 %while.35 = (s32[]{:T(128)}, f32[2,2,480,128]{3,2,1,0:T(8,128)}, f32[1280,4,512]{2,1,0:T(4,128)}, s32[5]{0:T(128)S(1)}, s32[2,8]{1,0:T(2,128)S(1)}, /*index=5*/b...) while((s32[]{:T(128)}, f32[2,2,480,128]{3,2,1,0:T(8,128)}, ...), condition=%wide.region_12.13_spmd.clone, body=%wide.region_10.12_spmd.clone.sunk | while | flops 1270183168 | bytes 55970532 | solution.py:291
  1188.3 177.0 %all-reduce.14 = bf16[1280,4,512]{2,1,0:T(4,128)(2,1)} all-reduce(f32[1280,4,512]{2,1,0:T(4,128)} %get-tuple-element.344), channel_id=3, replica_groups=mesh['ctx'=4,'fsdp'=8] {'ctx','fsdp'}, use_global_device_ids=true, to_apply=%region_13.14.clone | all-reduce | flops 2621440 | bytes 15728640
  1381.3 23.8 convolution_convert_fusion
  1405.1 44.4 %pad_maximum_fusion = bf16[1536,21504]{1,0:T(8,128)(2,1)} fusion(bf16[1536,1536]{1,0:T(8,128)(2,1)} %convolution_convert_fusion.3, bf16[1536,2048]{1,0:T(8,128)(2,1)} %convolution_convert_fusion.2, bf16[1536,17920]{1,0:T(8,128)(2,1)} %convolution_convert_fusion), kind=kLoop, calls=%fused_computation.73 | loop fusion | flops 198180864 | bytes 132120576 | tf_op jit(solution)/shard_map/concatenate | solution.py:314
  1450.1 628.3 %reduce-scatter.3.cloned.1.call-done = bf16[192,21504]{1,0:T(8,128)(2,1)} async-done(((bf16[1536,21504]{1,0:T(8,128)(2,1)}), bf16[192,21504]{1,0:T(8,128)(2,1)}) %reduce-scatter.3.cloned.1.call-update) | async-done | bytes 8257552 | tf_op jit(solution)/shard_map/reduce_scatter | solution.py:313
  2080.5 16.2 fusion.44
  2106.5 26.1 %all-reduce.7 = (bf16[1536]{0:T(1024)(128)(2,1)S(1)}, bf16[1792]{0:T(1024)(128)(2,1)S(1)}, bf16[256]{0:T(256)(128)(2,1)S(1)}, bf16[1536]{0:T(1024)(128)(2,1)S(1)}) all-reduce(f32[1536]{0:T(1024)S(1)} %get-tuple-element.419, f32[1792]{0:T(1024)S(1)} %bitcast.255, ...), channel_id=4, replica_groups=mesh['ctx'=4,'fsdp'=8] {'fsdp'}, use_global_device_ids=true, to_apply=%region_16.17.clone | all-reduce | flops 5120 | bytes 30720
  2145.7 26.4 %all-reduce.13.cloned.1.call-done = bf16[1120,1536]{1,0:T(8,128)(2,1)} async-done(((bf16[1120,1536]{1,0:T(8,128)(2,1)}), bf16[1120,1536]{1,0:T(8,128)(2,1)}) %all-reduce.13.cloned.1.call-update) | async-done | bytes 3440656 | tf_op jit(solution)/shard_map/psum | solution.py:351
  2177.9 288.8 %all-gather.25.cloned.1.call-done = bf16[768,21504]{1,0:T(8,128)(2,1)} async-done(((bf16[192,21504]{1,0:T(8,128)(2,1)}), bf16[768,21504]{1,0:T(8,128)(2,1)}) %all-gather.25.cloned.1.call-update) | async-done | bytes 33030160 | tf_op jit(solution)/shard_map/all_gather | solution.py:25
  2466.7 16.1 reduce_sum.139
  (514 shorter events, 365.2 us)
Async XLA Ops:
  7.2 70.4 %all-gather.11.cloned.1.call-start = ((), (), s32[]{:S(2)}) async-start(), calls=%async_computation.2 | async-start | bytes 7077888 | tf_op jit(solution)/shard_map/all_gather | solution.py:130
  7.9 98.2 %all-gather.13.cloned.1.call-start = ((), (), s32[]{:S(2)}) async-start(), calls=%async_computation.3 | async-start | bytes 1474560 | tf_op jit(solution)/shard_map/all_gather | solution.py:158
  9.1 72.6 %copy-start = (f32[160,1536]{1,0:T(8,128)}, f32[160,1536]{1,0:T(8,128)S(1)}, u32[]{:S(2)}) copy-start(f32[160,1536]{1,0:T(8,128)S(1)} %reshape.608) | copy-start | bytes 2949124
  42.6 39.1 %copy-start.28 = (f32[1536]{0:T(1024)}, f32[1536]{0:T(1024)S(1)}, u32[]{:S(2)}) copy-start(f32[1536]{0:T(1024)S(1)} %convert_element_type.153) | copy-start | bytes 18436
  44.1 33.6 %copy-start.31 = (f32[160]{0:T(256)}, f32[160]{0:T(256)S(1)}, u32[]{:S(2)}) copy-start(f32[160]{0:T(256)S(1)} %rsqrt.20) | copy-start | bytes 1924
  45.6 36.7 %copy-start.25 = (f32[160,128]{1,0:T(8,128)}, f32[160,128]{1,0:T(8,128)S(1)}, u32[]{:S(2)}) copy-start(f32[160,128]{1,0:T(8,128)S(1)} %pad_maximum_fusion.4) | copy-start | bytes 245764
  46.4 35.7 %copy-start.23 = (f32[160,128]{1,0:T(8,128)}, f32[160,128]{1,0:T(8,128)S(1)}, u32[]{:S(2)}) copy-start(f32[160,128]{1,0:T(8,128)S(1)} %get-tuple-element.499) | copy-start | bytes 245764
  81.7 25.7 %copy-start.13 = (f32[160,2048]{1,0:T(8,128)}, f32[160,2048]{1,0:T(8,128)S(1)}, u32[]{:S(2)}) copy-start(f32[160,2048]{1,0:T(8,128)S(1)} %convolution_add_fusion.4) | copy-start | bytes 3932164
  83.9 84.9 %all-gather.15.cloned.1.call-start = ((), (), s32[]{:S(2)}) async-start(), calls=%async_computation.4 | async-start | bytes 6553600 | tf_op jit(solution)/shard_map/all_gather | solution.py:183
  106.1 147.5 %all-gather.17.cloned.1.call-start = ((), (), s32[]{:S(2)}) async-start(), calls=%async_computation.5 | async-start | bytes 5308416 | tf_op jit(solution)/shard_map/all_gather | solution.py:131
  106.7 354.3 %all-gather.19.cloned.1.call-start = ((), (), s32[]{:S(2)}) async-start(), calls=%async_computation.6 | async-start | bytes 30965760 | tf_op jit(solution)/shard_map/all_gather | solution.py:211
  107.3 592.6 %all-gather.21.cloned.1.call-start = ((), (), s32[]{:S(2)}) async-start(), calls=%async_computation.7 | async-start | bytes 30965760 | tf_op jit(solution)/shard_map/all_gather | solution.py:212
  107.9 831.1 %all-gather.23.cloned.1.call-start = ((), (), s32[]{:S(2)}) async-start(), calls=%async_computation.8 | async-start | bytes 30965760 | tf_op jit(solution)/shard_map/all_gather | solution.py:213
  108.7 1340.9 %reduce-scatter.5.cloned.1.call-start = ((), (), s32[]{:S(2)}) async-start(), calls=%async_computation.10 | async-start | bytes 30965760 | tf_op jit(solution)/shard_map/reduce_scatter | solution.py:335
  116.4 7.4 copy-start.15
  122.0 46.8 %copy-start.30 = (s32[2,8]{1,0:T(2,128)S(1)}, s32[2,8]{1,0:T(2,128)}, u32[]{:S(2)}) copy-start(s32[2,8]{1,0:T(2,128)} %param.16) | copy-start | bytes 196
  257.2 750.0 %copy-start.7 = (f32[160,1536]{1,0:T(8,128)}, f32[160,1536]{1,0:T(8,128)S(1)}, u32[]{:S(2)}) copy-start(f32[160,1536]{1,0:T(8,128)S(1)} %get-tuple-element.511) | copy-start | bytes 2949124
  257.4 442.5 %copy-start.9 = (bf16[160,1536]{1,0:T(8,128)(2,1)}, bf16[160,1536]{1,0:T(8,128)(2,1)S(1)}, u32[]{:S(2)}) copy-start(bf16[160,1536]{1,0:T(8,128)(2,1)S(1)} %multiply_convert_fusion.3) | copy-start | bytes 1474564
  477.3 461.7 %copy-start.16 = (bf16[160,1536]{1,0:T(8,128)(2,1)S(1)}, bf16[160,1536]{1,0:T(8,128)(2,1)}, u32[]{:S(2)}) copy-start(bf16[160,1536]{1,0:T(8,128)(2,1)} %reshape.600) | copy-start | bytes 1474564
  974.0 1104.4 %reduce-scatter.3.cloned.1.call-start = ((), (), s32[]{:S(2)}) async-start(), calls=%async_computation.9 | async-start | bytes 74317824 | tf_op jit(solution)/shard_map/reduce_scatter | solution.py:313
  1008.4 5.8 copy-start.17
  1370.4 5.8 copy-start.22
  1449.5 722.6 %all-reduce.13.cloned.1.call-start = ((), (), s32[]{:S(2)}) async-start(), calls=%async_computation.11 | async-start | bytes 6881280 | tf_op jit(solution)/shard_map/psum | solution.py:351
  1450.1 1016.6 %all-gather.25.cloned.1.call-start = ((), (), s32[]{:S(2)}) async-start(), calls=%async_computation.12 | async-start | bytes 41287680 | tf_op jit(solution)/shard_map/all_gather | solution.py:25
  (29 other events, 90.2 us)
Sparse Core Ops, SparseCore 0:
  9.6 67.9 all-gather.10
  84.0 22.0 all-gather.12
  108.0 60.8 all-gather.14
  170.3 51.1 all-gather.16
  223.1 237.9 all-gather.18
  462.5 237.3 all-gather.20
  701.6 237.3 all-gather.22
  974.1 267.4 reduce-scatter.4
  1449.6 628.7 reduce-scatter.2
  2081.5 90.5 all-reduce.12
  2174.0 292.7 all-gather.24
